TPU v7x, 32 devices: a whole 2x2x4 slice. The times are simulated.
32 devices in a mesh: trial: 4 (over x, core), north: 2 (over y), east: 4 (over z).
Axes of the slice: x: 2, y: 2, z: 4, core: 2. Of those that a mesh axis runs over, the one named last changes fastest.
Arguments:
- pair_state: bfloat16 [192, 48, 128], P(('trial', 'north'), 'east'), parts along dimension 0, may hold values from -6 to 6
- in_gain: float32 [128], replicated, may hold values from 0.25 to 1.75
- left_weight: bfloat16 [512, 128], P('trial'), parts along dimension 0, may hold values from -0.5 to 0.5
- right_weight: bfloat16 [512, 128], P('trial'), parts along dimension 0, may hold values from -0.5 to 0.5
- left_gate: bfloat16 [512, 128], P('trial'), parts along dimension 0, may hold values from -0.5 to 0.5
- right_gate: bfloat16 [512, 128], P('trial'), parts along dimension 0, may hold values from -0.5 to 0.5
- mid_gain: float32 [128], replicated, may hold values from 0.25 to 1.75
- out_weight: bfloat16 [512, 128], P('trial'), parts along dimension 0, may hold values from -0.5 to 0.5
- out_gate: bfloat16 [512, 128], P('trial'), parts along dimension 0, may hold values from -0.5 to 0.5
Outputs:
- triangle_out: bfloat16 [192, 48, 128], P(('trial', 'north'), 'east'), parts along dimension 0
There are 4 independent parts, one for each index of `trial`. A program takes and returns all parts, laid end to end along the dimension named above; an argument that names none is the same for every part. Nothing has to cross between parts.
All inputs are finite; a program needn't handle non-finite values.
Results may differ from a plain program's by a relative error of at most 0.015.
Values may be sent and summed in bfloat16 or wider, within the bound.
A program may use at most 64 MiB of HBM per device.

v0:
```python
import jax
import jax.numpy as jnp
from jax import lax
from jax.sharding import PartitionSpec as P


def norm_channels(values, channel_gain):
    centred = values - jnp.mean(values, axis=-1, keepdims=True)
    return (
        centred
        * lax.rsqrt(jnp.mean(centred * centred, axis=-1, keepdims=True) + 1e-05)
        * channel_gain
    )


def make_factors(pair_in, in_gain, left_weight, right_weight, left_gate, right_gate):
    ready = norm_channels(pair_in.astype(jnp.float32), in_gain).astype(jnp.bfloat16)
    ready = lax.optimization_barrier(ready)
    left = jnp.einsum("ijc,cd->ijd", ready, left_weight, preferred_element_type=jnp.float32)
    left = left * jax.nn.sigmoid(
        jnp.einsum("ijc,cd->ijd", ready, left_gate, preferred_element_type=jnp.float32)
    )
    right = jnp.einsum("ijc,cd->ijd", ready, right_weight, preferred_element_type=jnp.float32)
    right = right * jax.nn.sigmoid(
        jnp.einsum("ijc,cd->ijd", ready, right_gate, preferred_element_type=jnp.float32)
    )
    return (ready, left.astype(jnp.bfloat16), right.astype(jnp.bfloat16))


def to_pair(mixed, ready, mid_gain, out_weight, out_gate):
    scaled = norm_channels(mixed.astype(jnp.float32), mid_gain).astype(jnp.bfloat16)
    scaled = lax.optimization_barrier(scaled)
    gate = jax.nn.sigmoid(
        jnp.einsum("ijc,cd->ijd", ready, out_gate, preferred_element_type=jnp.float32)
    )
    return (
        jnp.einsum("ijd,dc->ijc", scaled, out_weight, preferred_element_type=jnp.float32) * gate
    ).astype(jnp.bfloat16)


def local(
    pair_state,
    in_gain,
    left_weight,
    right_weight,
    left_gate,
    right_gate,
    mid_gain,
    out_weight,
    out_gate,
):
    ready, left, right = make_factors(
        pair_state, in_gain, left_weight, right_weight, left_gate, right_gate
    )
    count = pair_state.shape[1] * lax.axis_size("east")
    left_lines, right_lines = (
        lax.all_to_all(left, "east", split_axis=2, concat_axis=1, tiled=True),
        lax.all_to_all(right, "east", split_axis=2, concat_axis=1, tiled=True),
    )
    strip = jnp.einsum(
        "ikd,jkd->ijd",
        left_lines,
        lax.all_gather(right_lines, "north", axis=0, tiled=True),
        preferred_element_type=jnp.float32,
    )
    strip = (strip * count ** (-0.5)).astype(jnp.bfloat16)
    mixed = lax.all_to_all(strip, "east", split_axis=1, concat_axis=2, tiled=True)
    return to_pair(mixed, ready, mid_gain, out_weight, out_gate)


def solution(mesh):
    return jax.shard_map(
        local,
        mesh=mesh,
        in_specs=(
            P(("trial", "north"), "east", None),
            P(),
            P("trial", None),
            P("trial", None),
            P("trial", None),
            P("trial", None),
            P(),
            P("trial", None),
            P("trial", None),
        ),
        out_specs=P(("trial", "north"), "east", None),
        check_vma=False,
    )
```

profile of v0, /device:TPU:0, one launch (start us, length us, event | category | flops | bytes accessed | tf_op | source)
XLA Modules:
  0.0 44.6 jit_solution(821063206014544712)
XLA Ops:
  0.0 1.1 %convert_reduce_fusion = f32[24,12]{0,1:T(8,128)S(1)} fusion(bf16[24,12,128]{2,0,1:T(8,128)(2,1)} %param.9), kind=kLoop, calls=%fused_computation.25 | loop fusion | flops 73440 | bytes 74880 | tf_op jit(solution)/shard_map/reduce_sum | solution.py:8
  1.3 0.6 %copy-done.4 = f32[128]{0:T(128)S(1)} copy-done((f32[128]{0:T(128)S(1)}, f32[128]{0:T(128)}, u32[]{:S(2)}) %copy-start.4) | copy-done | bytes 536
  2.3 0.6 %copy-done.6 = bf16[128,128]{1,0:T(8,128)(2,1)S(1)} copy-done((bf16[128,128]{1,0:T(8,128)(2,1)S(1)}, bf16[128,128]{1,0:T(8,128)(2,1)}, u32[]{:S(2)}) %copy-start.6) | copy-done | bytes 32792
  2.9 0.2 fusion.16
  3.1 0.4 copy.34
  3.5 1.1 %reshape.41 = bf16[4,2,4608]{2,1,0:T(2,128)(2,1)} reshape(bf16[128,12,24]{2,1,0:T(8,128)(2,1)S(1)} %bitcast.55) | data formatting | bytes 147456
  4.7 6.5 %all-to-all-start = ((bf16[4,2,4608]{2,1,0:T(2,128)(2,1)}), bf16[4,2,4608]{2,1,0:T(2,128)(2,1)S(1)}, u32[]{:S(2)}, u32[]{:S(2)}) async-start(bf16[4,2,4608]{2,1,0:T(2,128)(2,1)} %reshape.41), calls=%async_computation | async-start | bytes 147456 | tf_op jit(solution)/shard_map/all_to_all | solution.py:58
  11.3 0.6 %copy-done.7 = bf16[128,128]{1,0:T(8,128)(2,1)S(1)} copy-done((bf16[128,128]{1,0:T(8,128)(2,1)S(1)}, bf16[128,128]{1,0:T(8,128)(2,1)}, u32[]{:S(2)}) %copy-start.7) | copy-done | bytes 32792
  11.9 0.2 fusion.15
  12.1 0.4 copy.37
  12.5 1.1 %reshape.43 = bf16[4,2,4608]{2,1,0:T(2,128)(2,1)} reshape(bf16[128,12,24]{2,1,0:T(8,128)(2,1)S(1)} %bitcast.56) | data formatting | bytes 147456
  13.7 3.2 %all-to-all-done = bf16[4,2,4608]{2,1,0:T(2,128)(2,1)S(1)} async-done(((bf16[4,2,4608]{2,1,0:T(2,128)(2,1)}), bf16[4,2,4608]{2,1,0:T(2,128)(2,1)S(1)}, u32[]{:S(2)}, u32[]{:S(2)}) %all-to-all-start) | async-done | bytes 73760 | tf_op jit(solution)/shard_map/all_to_all | solution.py:58
  16.9 3.3 %all-to-all-start.1 = ((bf16[4,2,4608]{2,1,0:T(2,128)(2,1)}), bf16[4,2,4608]{2,1,0:T(2,128)(2,1)S(1)}, u32[]{:S(2)}, u32[]{:S(2)}) async-start(bf16[4,2,4608]{2,1,0:T(2,128)(2,1)} %reshape.43), calls=%async_computation.1 | async-start | bytes 147456 | tf_op jit(solution)/shard_map/all_to_all | solution.py:57
  20.2 0.6 %reshape.42 = bf16[128,12,24]{2,1,0:T(8,128)(2,1)S(1)} reshape(bf16[4,2,4608]{2,1,0:T(2,128)(2,1)S(1)} %all-to-all-done) | data formatting | bytes 147456
  20.8 0.4 copy.35
  21.2 0.3 copy.36
  21.5 6.3 %all_gather.3 = bf16[48,48,32]{1,0,2:T(8,128)(2,1)S(1)} all-gather(bf16[24,48,32]{1,0,2:T(8,128)(2,1)S(1)} %copy.36), channel_id=1, replica_groups=mesh['trial'=4,'north'=2,'east'=4] {'north'}, dimensions={0}, use_global_device_ids=true | all-gather | bytes 221184 | tf_op jit(solution)/shard_map/all_gather | solution.py:63
  27.8 0.6 %reshape.44 = bf16[128,12,24]{2,1,0:T(8,128)(2,1)S(1)} reshape(bf16[4,2,4608]{2,1,0:T(2,128)(2,1)S(1)} %all-to-all-done.1) | data formatting | bytes 147456
  28.4 0.4 copy.38
  28.8 0.3 copy.39
  29.1 0.3 fusion.1
  29.4 0.2 copy.40
  29.6 0.3 reshape.45
  29.9 10.6 %all_to_all.45 = bf16[4,2,4608]{2,1,0:T(2,128)(2,1)S(1)} all-to-all(bf16[4,2,4608]{2,1,0:T(2,128)(2,1)S(1)} %reshape.45), channel_id=1, replica_groups=mesh['trial'=4,'north'=2,'east'=4] {'east'}, dimensions={0} | all-to-all | bytes 147456 | tf_op jit(solution)/shard_map/all_to_all | solution.py:67
  40.5 0.2 reshape.46
  40.9 0.2 multiply_reduce_fusion
  41.2 0.4 copy.41
  41.6 0.3 reshape.32
  41.9 0.4 copy-done.5
  42.4 0.6 %copy-done.3 = bf16[128,128]{1,0:T(8,128)(2,1)S(1)} copy-done((bf16[128,128]{1,0:T(8,128)(2,1)S(1)}, bf16[128,128]{1,0:T(8,128)(2,1)}, u32[]{:S(2)}) %copy-start.3) | copy-done | bytes 32792
  43.2 0.6 %copy-done.8 = bf16[128,128]{1,0:T(8,128)(2,1)S(1)} copy-done((bf16[128,128]{1,0:T(8,128)(2,1)S(1)}, bf16[128,128]{1,0:T(8,128)(2,1)}, u32[]{:S(2)}) %copy-start.8) | copy-done | bytes 32792
  43.7 0.8 %fusion.14 = bf16[24,12,128]{2,0,1:T(8,128)(2,1)} fusion(f32[24,12,128]{2,0,1:T(8,128)S(1)} %fusion.24, bf16[24,12,128]{2,0,1:T(8,128)(2,1)S(1)} %fusion.22, bf16[128,128]{1,0:T(8,128)(2,1)S(1)} %copy-done.8), kind=kOutput, calls=%fused_computation.18 | convolution fusion | flops 9621504 | bytes 327680 | tf_op jit(solution)/shard_map/ijc,cd->ijd/dot_general | solution.py:34
  (25 shorter events, 1.2 us)
Async XLA Ops:
  0.0 2.1 %copy-start = (bf16[128,128]{1,0:T(8,128)(2,1)S(1)}, bf16[128,128]{1,0:T(8,128)(2,1)}, u32[]{:S(2)}) copy-start(bf16[128,128]{1,0:T(8,128)(2,1)} %param.12) | copy-start | bytes 98308
  0.0 1.1 %copy-start.1 = (bf16[24,12,128]{2,0,1:T(8,128)(2,1)S(1)}, bf16[24,12,128]{2,0,1:T(8,128)(2,1)}, u32[]{:S(2)}) copy-start(bf16[24,12,128]{2,0,1:T(8,128)(2,1)} %param.9) | copy-start | bytes 221188
  1.3 0.7 %copy-start.4 = (f32[128]{0:T(128)S(1)}, f32[128]{0:T(128)}, u32[]{:S(2)}) copy-start(f32[128]{0:T(128)} %param.10) | copy-start | bytes 1540
  2.1 0.8 %copy-start.6 = (bf16[128,128]{1,0:T(8,128)(2,1)S(1)}, bf16[128,128]{1,0:T(8,128)(2,1)}, u32[]{:S(2)}) copy-start(bf16[128,128]{1,0:T(8,128)(2,1)} %param.14) | copy-start | bytes 98308
  4.7 6.5 %copy-start.2 = (bf16[128,128]{1,0:T(8,128)(2,1)S(1)}, bf16[128,128]{1,0:T(8,128)(2,1)}, u32[]{:S(2)}) copy-start(bf16[128,128]{1,0:T(8,128)(2,1)} %param.11) | copy-start | bytes 98308
  4.7 12.2 %all-to-all-start = ((bf16[4,2,4608]{2,1,0:T(2,128)(2,1)}), bf16[4,2,4608]{2,1,0:T(2,128)(2,1)S(1)}, u32[]{:S(2)}, u32[]{:S(2)}) async-start(bf16[4,2,4608]{2,1,0:T(2,128)(2,1)} %reshape.41), calls=%async_computation | async-start | bytes 147456 | tf_op jit(solution)/shard_map/all_to_all | solution.py:58
  11.1 0.8 %copy-start.7 = (bf16[128,128]{1,0:T(8,128)(2,1)S(1)}, bf16[128,128]{1,0:T(8,128)(2,1)}, u32[]{:S(2)}) copy-start(bf16[128,128]{1,0:T(8,128)(2,1)} %param.13) | copy-start | bytes 98308
  16.9 10.9 %all-to-all-start.1 = ((bf16[4,2,4608]{2,1,0:T(2,128)(2,1)}), bf16[4,2,4608]{2,1,0:T(2,128)(2,1)S(1)}, u32[]{:S(2)}, u32[]{:S(2)}) async-start(bf16[4,2,4608]{2,1,0:T(2,128)(2,1)} %reshape.43), calls=%async_computation.1 | async-start | bytes 147456 | tf_op jit(solution)/shard_map/all_to_all | solution.py:57
  41.6 0.7 %copy-start.5 = (f32[128]{0:T(128)S(1)}, f32[128]{0:T(128)}, u32[]{:S(2)}) copy-start(f32[128]{0:T(128)} %param.15) | copy-start | bytes 1540
  42.2 0.8 %copy-start.3 = (bf16[128,128]{1,0:T(8,128)(2,1)S(1)}, bf16[128,128]{1,0:T(8,128)(2,1)}, u32[]{:S(2)}) copy-start(bf16[128,128]{1,0:T(8,128)(2,1)} %param.16) | copy-start | bytes 98308
  43.0 0.8 %copy-start.8 = (bf16[128,128]{1,0:T(8,128)(2,1)S(1)}, bf16[128,128]{1,0:T(8,128)(2,1)}, u32[]{:S(2)}) copy-start(bf16[128,128]{1,0:T(8,128)(2,1)} %param.17) | copy-start | bytes 98308
where the time goes:
time: 45.3 us; the launch traced here: 44.6 us
  blocking collectives  17 us (38%)
  local copies, waits for them, and re-layouts  10.4 us (23%)
  starting transfers between devices  9.77 us (22%)
  waiting for transfers between devices  3.24 us (7%)
  matrix products  2.02 us (4%)
  other arithmetic  1.96 us (4%)
    all_to_all x1, blocking collectives, local(): lax.all_to_all(strip, 'east', split_axis=1, concat_axis=2, tiled=True)  10.6 us
    unnamed x24, local copies, waits for them, and re-layouts  7.31 us
    all_to_all x1, starting transfers between devices, local(): lax.all_to_all(right, 'east', split_axis=2, concat_axis=1, tiled=True)  6.48 us
    all_gather x1, blocking collectives, local(): lax.all_gather(right_lines, 'north', axis=0, tiled=True)  6.34 us
    all_to_all x1, starting transfers between devices, local(): lax.all_to_all(left, 'east', split_axis=2, concat_axis=1, tiled=True)  3.29 us
    all_to_all x1, waiting for transfers between devices, local(): lax.all_to_all(right, 'east', split_axis=2, concat_axis=1, tiled=True)  3.23 us
    reduce_sum x2, other arithmetic, norm_channels(): centred = values - jnp.mean(values, axis=-1, keepdims=True)  1.19 us
  transfers between devices with their start and end apart: 2, of which 1 were waited for; matrix products, arithmetic and copies ran while one was open for 7% of the time, Pallas kernels for 0%

commit v1 on v0

--- a/solution.py
+++ b/solution.py
@@ -2,6 +2,21 @@
 import jax.numpy as jnp
 from jax import lax
 from jax.sharding import PartitionSpec as P
+
+
+def work_around(array, axis, dim, make, out_dim):
+    ways, here, step = (lax.axis_size(axis), lax.axis_index(axis), array.shape[dim])
+    results = []
+    for far in range(ways):
+        arriving = (
+            lax.ppermute(array, axis, [(d, (d + 1) % ways) for d in range(ways)])
+            if far + 1 < ways
+            else array
+        )
+        results.append(make(array, (here - far) % ways * step))
+        array = arriving
+    line = jnp.concatenate(results[::-1], axis=out_dim)
+    return jnp.roll(line, (here + 1) * results[0].shape[out_dim], axis=out_dim)
 
 
 def norm_channels(values, channel_gain):
@@ -57,11 +72,14 @@
         lax.all_to_all(left, "east", split_axis=2, concat_axis=1, tiled=True),
         lax.all_to_all(right, "east", split_axis=2, concat_axis=1, tiled=True),
     )
-    strip = jnp.einsum(
-        "ikd,jkd->ijd",
-        left_lines,
-        lax.all_gather(right_lines, "north", axis=0, tiled=True),
-        preferred_element_type=jnp.float32,
+    strip = work_around(
+        right_lines,
+        "north",
+        0,
+        lambda own_block, offset: jnp.einsum(
+            "ikd,jkd->ijd", left_lines, own_block, preferred_element_type=jnp.float32
+        ),
+        1,
     )
     strip = (strip * count ** (-0.5)).astype(jnp.bfloat16)
     mixed = lax.all_to_all(strip, "east", split_axis=1, concat_axis=2, tiled=True)

time: 45.3 us -> 43.8 us (0.967)
  blocking collectives: 17 us -> 10.4 us
  waiting for transfers between devices: 3.24 us -> 6.09 us
  starting transfers between devices: 9.77 us -> 11.4 us
  other arithmetic: 1.96 us -> 2.45 us
    all_gather x1 -> x0, blocking collectives: 6.34 us -> none  [local(): lax.all_gather(right_lines, 'north', axis=0, tiled=True)]
    all_to_all x1, waiting for transfers between devices: 0.01 us -> 2.86 us  [local(): lax.all_to_all(left, 'east', split_axis=2, concat_axis=1, tiled=True)]
    ppermute x0 -> x1, starting transfers between devices: none -> 1.58 us  [work_around(): lax.ppermute(array, axis, [(d, (d + 1) % ways) for d in range(ways)])]
    convert_element_type x0 -> x1, other arithmetic: none -> 0.49 us  [local(): strip = (strip * count ** (-0.5)).astype(jnp.bfloat16)]
  transfers between devices with their start and end apart: 2 -> 3, of which waited for: 1 -> 2; matrix products, arithmetic and copies ran while one was open for 7% -> 11% of each run, Pallas kernels for 0% -> 0%
where the time goes in v1:
time: 43.8 us; the launch traced here: 43.1 us
  starting transfers between devices  11.4 us (26%)
  local copies, waits for them, and re-layouts  10.4 us (24%)
  blocking collectives  10.4 us (24%)
  waiting for transfers between devices  6.09 us (14%)
  other arithmetic  2.45 us (6%)
  matrix products  2.16 us (5%)
    all_to_all x1, blocking collectives, local(): lax.all_to_all(strip, 'east', split_axis=1, concat_axis=2, tiled=True)  10.4 us
    unnamed x24, local copies, waits for them, and re-layouts  7.32 us
    all_to_all x1, starting transfers between devices, local(): lax.all_to_all(right, 'east', split_axis=2, concat_axis=1, tiled=True)  6.48 us
    all_to_all x1, starting transfers between devices, local(): lax.all_to_all(left, 'east', split_axis=2, concat_axis=1, tiled=True)  3.29 us
    all_to_all x1, waiting for transfers between devices, local(): lax.all_to_all(right, 'east', split_axis=2, concat_axis=1, tiled=True)  3.23 us
    all_to_all x1, waiting for transfers between devices, local(): lax.all_to_all(left, 'east', split_axis=2, concat_axis=1, tiled=True)  2.86 us
    ppermute x1, starting transfers between devices, work_around(): lax.ppermute(array, axis, [(d, (d + 1) % ways) for d in range(ways)])  1.58 us
    reduce_sum x2, other arithmetic, norm_channels(): centred = values - jnp.mean(values, axis=-1, keepdims=True)  1.19 us
  transfers between devices with their start and end apart: 3, of which 2 were waited for; matrix products, arithmetic and copies ran while one was open for 11% of the time, Pallas kernels for 0%

profile of v1, /device:TPU:0, one launch (start us, length us, event | category | flops | bytes accessed | tf_op | source)
XLA Modules:
  0.0 43.1 jit_solution(13318891484329323369)
XLA Ops:
  0.0 1.1 %convert_reduce_fusion = f32[24,12]{0,1:T(8,128)S(1)} fusion(bf16[24,12,128]{2,0,1:T(8,128)(2,1)} %param.9), kind=kLoop, calls=%fused_computation.29 | loop fusion | flops 73440 | bytes 74880 | tf_op jit(solution)/shard_map/reduce_sum | solution.py:23
  1.3 0.6 %copy-done.4 = f32[128]{0:T(128)S(1)} copy-done((f32[128]{0:T(128)S(1)}, f32[128]{0:T(128)}, u32[]{:S(2)}) %copy-start.4) | copy-done | bytes 536
  2.3 0.6 %copy-done.6 = bf16[128,128]{1,0:T(8,128)(2,1)S(1)} copy-done((bf16[128,128]{1,0:T(8,128)(2,1)S(1)}, bf16[128,128]{1,0:T(8,128)(2,1)}, u32[]{:S(2)}) %copy-start.6) | copy-done | bytes 32792
  3.1 0.4 copy.40
  3.5 1.1 %reshape.41 = bf16[4,2,4608]{2,1,0:T(2,128)(2,1)} reshape(bf16[128,12,24]{2,1,0:T(8,128)(2,1)S(1)} %bitcast.59) | data formatting | bytes 147456
  4.7 6.5 %all-to-all-start = ((bf16[4,2,4608]{2,1,0:T(2,128)(2,1)}), bf16[4,2,4608]{2,1,0:T(2,128)(2,1)S(1)}, u32[]{:S(2)}, u32[]{:S(2)}) async-start(bf16[4,2,4608]{2,1,0:T(2,128)(2,1)} %reshape.41), calls=%async_computation | async-start | bytes 147456 | tf_op jit(solution)/shard_map/all_to_all | solution.py:73
  11.3 0.6 %copy-done.7 = bf16[128,128]{1,0:T(8,128)(2,1)S(1)} copy-done((bf16[128,128]{1,0:T(8,128)(2,1)S(1)}, bf16[128,128]{1,0:T(8,128)(2,1)}, u32[]{:S(2)}) %copy-start.7) | copy-done | bytes 32792
  12.1 0.4 copy.43
  12.5 1.1 %reshape.43 = bf16[4,2,4608]{2,1,0:T(2,128)(2,1)} reshape(bf16[128,12,24]{2,1,0:T(8,128)(2,1)S(1)} %bitcast.60) | data formatting | bytes 147456
  13.7 3.2 %all-to-all-done = bf16[4,2,4608]{2,1,0:T(2,128)(2,1)S(1)} async-done(((bf16[4,2,4608]{2,1,0:T(2,128)(2,1)}), bf16[4,2,4608]{2,1,0:T(2,128)(2,1)S(1)}, u32[]{:S(2)}, u32[]{:S(2)}) %all-to-all-start) | async-done | bytes 73760 | tf_op jit(solution)/shard_map/all_to_all | solution.py:73
  16.9 3.3 %all-to-all-start.1 = ((bf16[4,2,4608]{2,1,0:T(2,128)(2,1)}), bf16[4,2,4608]{2,1,0:T(2,128)(2,1)S(1)}, u32[]{:S(2)}, u32[]{:S(2)}) async-start(bf16[4,2,4608]{2,1,0:T(2,128)(2,1)} %reshape.43), calls=%async_computation.1 | async-start | bytes 147456 | tf_op jit(solution)/shard_map/all_to_all | solution.py:72
  20.2 0.6 %reshape.42 = bf16[128,12,24]{2,1,0:T(8,128)(2,1)S(1)} reshape(bf16[4,2,4608]{2,1,0:T(2,128)(2,1)S(1)} %all-to-all-done) | data formatting | bytes 147456
  20.8 0.4 copy.41
  21.2 0.3 copy.42
  21.5 1.6 %collective-permute-start = (bf16[24,48,32]{1,0,2:T(8,128)(2,1)S(1)}, bf16[24,48,32]{1,0,2:T(8,128)(2,1)S(1)}, u32[]{:S(2)}, u32[]{:S(2)}) collective-permute-start(bf16[24,48,32]{1,0,2:T(8,128)(2,1)S(1)} %copy.42), channel_id=1, source_target_pairs={{0,4},{4,0},{1,5},{5,1},{2,6},{6,2},{3,7},{7,3},{8,12},{12,8},{9,1... | collective-permute-start | bytes 221192 | tf_op jit(solution)/shard_map/ppermute | solution.py:12
  23.1 2.9 %all-to-all-done.1 = bf16[4,2,4608]{2,1,0:T(2,128)(2,1)S(1)} async-done(((bf16[4,2,4608]{2,1,0:T(2,128)(2,1)}), bf16[4,2,4608]{2,1,0:T(2,128)(2,1)S(1)}, u32[]{:S(2)}, u32[]{:S(2)}) %all-to-all-start.1) | async-done | bytes 73760 | tf_op jit(solution)/shard_map/all_to_all | solution.py:72
  25.9 0.6 %reshape.44 = bf16[128,12,24]{2,1,0:T(8,128)(2,1)S(1)} reshape(bf16[4,2,4608]{2,1,0:T(2,128)(2,1)S(1)} %all-to-all-done.1) | data formatting | bytes 147456
  26.5 0.4 copy.44
  26.9 0.3 copy.45
  27.2 0.2 convolution_bitcast_fusion
  27.4 0.2 convolution_bitcast_fusion.1
  27.7 0.5 %fusion.16 = bf16[24,48,32]{1,0,2:T(8,128)(2,1)S(1)} fusion(s32[]{:T(128)S(6)} %select_n.14, f32[24,24,32]{1,0,2:T(8,128)S(1)} %convolution_bitcast_fusion, f32[24,24,32]{1,0,2:T(8,128)S(1)} %convolution_bitcast_fusion.1), kind=kLoop, calls=%fused_computation.24 | loop fusion | flops 184320 | bytes 221188 | tf_op jit(solution)/shard_map/convert_element_type | solution.py:84
  28.2 0.2 copy.48
  28.4 0.3 reshape.45
  28.7 10.4 %all_to_all.45 = bf16[4,2,4608]{2,1,0:T(2,128)(2,1)S(1)} all-to-all(bf16[4,2,4608]{2,1,0:T(2,128)(2,1)S(1)} %reshape.45), channel_id=1, replica_groups=mesh['trial'=4,'north'=2,'east'=4] {'east'}, dimensions={0} | all-to-all | bytes 147456 | tf_op jit(solution)/shard_map/all_to_all | solution.py:85
  39.5 0.2 multiply_reduce_fusion
  39.7 0.4 copy.49
  40.1 0.3 reshape.32
  40.4 0.4 copy-done.5
  40.9 0.6 %copy-done.3 = bf16[128,128]{1,0:T(8,128)(2,1)S(1)} copy-done((bf16[128,128]{1,0:T(8,128)(2,1)S(1)}, bf16[128,128]{1,0:T(8,128)(2,1)}, u32[]{:S(2)}) %copy-start.3) | copy-done | bytes 32792
  41.7 0.6 %copy-done.8 = bf16[128,128]{1,0:T(8,128)(2,1)S(1)} copy-done((bf16[128,128]{1,0:T(8,128)(2,1)S(1)}, bf16[128,128]{1,0:T(8,128)(2,1)}, u32[]{:S(2)}) %copy-start.8) | copy-done | bytes 32792
  42.3 0.8 %fusion.12 = bf16[24,12,128]{2,0,1:T(8,128)(2,1)} fusion(f32[24,12,128]{2,0,1:T(8,128)S(1)} %fusion.24, bf16[24,12,128]{2,0,1:T(8,128)(2,1)S(1)} %fusion.22, bf16[128,128]{1,0:T(8,128)(2,1)S(1)} %copy-done.8), kind=kOutput, calls=%fused_computation.17 | convolution fusion | flops 9621504 | bytes 327680 | tf_op jit(solution)/shard_map/ijc,cd->ijd/dot_general | solution.py:49
  (28 shorter events, 1.8 us)
Async XLA Ops:
  0.0 2.1 %copy-start = (bf16[128,128]{1,0:T(8,128)(2,1)S(1)}, bf16[128,128]{1,0:T(8,128)(2,1)}, u32[]{:S(2)}) copy-start(bf16[128,128]{1,0:T(8,128)(2,1)} %param.12) | copy-start | bytes 98308
  0.0 1.1 %copy-start.1 = (bf16[24,12,128]{2,0,1:T(8,128)(2,1)S(1)}, bf16[24,12,128]{2,0,1:T(8,128)(2,1)}, u32[]{:S(2)}) copy-start(bf16[24,12,128]{2,0,1:T(8,128)(2,1)} %param.9) | copy-start | bytes 221188
  1.3 0.7 %copy-start.4 = (f32[128]{0:T(128)S(1)}, f32[128]{0:T(128)}, u32[]{:S(2)}) copy-start(f32[128]{0:T(128)} %param.10) | copy-start | bytes 1540
  2.1 0.8 %copy-start.6 = (bf16[128,128]{1,0:T(8,128)(2,1)S(1)}, bf16[128,128]{1,0:T(8,128)(2,1)}, u32[]{:S(2)}) copy-start(bf16[128,128]{1,0:T(8,128)(2,1)} %param.14) | copy-start | bytes 98308
  4.7 6.5 %copy-start.2 = (bf16[128,128]{1,0:T(8,128)(2,1)S(1)}, bf16[128,128]{1,0:T(8,128)(2,1)}, u32[]{:S(2)}) copy-start(bf16[128,128]{1,0:T(8,128)(2,1)} %param.11) | copy-start | bytes 98308
  4.7 12.2 %all-to-all-start = ((bf16[4,2,4608]{2,1,0:T(2,128)(2,1)}), bf16[4,2,4608]{2,1,0:T(2,128)(2,1)S(1)}, u32[]{:S(2)}, u32[]{:S(2)}) async-start(bf16[4,2,4608]{2,1,0:T(2,128)(2,1)} %reshape.41), calls=%async_computation | async-start | bytes 147456 | tf_op jit(solution)/shard_map/all_to_all | solution.py:73
  11.1 0.8 %copy-start.7 = (bf16[128,128]{1,0:T(8,128)(2,1)S(1)}, bf16[128,128]{1,0:T(8,128)(2,1)}, u32[]{:S(2)}) copy-start(bf16[128,128]{1,0:T(8,128)(2,1)} %param.13) | copy-start | bytes 98308
  16.9 9.0 %all-to-all-start.1 = ((bf16[4,2,4608]{2,1,0:T(2,128)(2,1)}), bf16[4,2,4608]{2,1,0:T(2,128)(2,1)S(1)}, u32[]{:S(2)}, u32[]{:S(2)}) async-start(bf16[4,2,4608]{2,1,0:T(2,128)(2,1)} %reshape.43), calls=%async_computation.1 | async-start | bytes 147456 | tf_op jit(solution)/shard_map/all_to_all | solution.py:72
  21.5 5.9 %collective-permute-start = (bf16[24,48,32]{1,0,2:T(8,128)(2,1)S(1)}, bf16[24,48,32]{1,0,2:T(8,128)(2,1)S(1)}, u32[]{:S(2)}, u32[]{:S(2)}) collective-permute-start(bf16[24,48,32]{1,0,2:T(8,128)(2,1)S(1)} %copy.42), channel_id=1, source_target_pairs={{0,4},{4,0},{1,5},{5,1},{2,6},{6,2},{3,7},{7,3},{8,12},{12,8},{9,1... | collective-permute-start | bytes 221192 | tf_op jit(solution)/shard_map/ppermute | solution.py:12
  40.1 0.7 %copy-start.5 = (f32[128]{0:T(128)S(1)}, f32[128]{0:T(128)}, u32[]{:S(2)}) copy-start(f32[128]{0:T(128)} %param.15) | copy-start | bytes 1540
  40.8 0.8 %copy-start.3 = (bf16[128,128]{1,0:T(8,128)(2,1)S(1)}, bf16[128,128]{1,0:T(8,128)(2,1)}, u32[]{:S(2)}) copy-start(bf16[128,128]{1,0:T(8,128)(2,1)} %param.16) | copy-start | bytes 98308
  41.5 0.8 %copy-start.8 = (bf16[128,128]{1,0:T(8,128)(2,1)S(1)}, bf16[128,128]{1,0:T(8,128)(2,1)}, u32[]{:S(2)}) copy-start(bf16[128,128]{1,0:T(8,128)(2,1)} %param.17) | copy-start | bytes 98308
